TPU v7x, 16 devices: a whole 2x2x2 slice. The times are simulated.
16 devices in a mesh: ga: 16 (over z, y, x, core).
Axes of the slice: x: 2, y: 2, z: 2, core: 2. Of those that a mesh axis runs over, the one named last changes fastest.
Arguments:
- text_states: bfloat16 [4096, 768], P('ga')
- text_proj: bfloat16 [768, 768], replicated
- gallery: bfloat16 [32768, 768], P('ga')
- logit_scale: float32 [1], replicated
Outputs:
- output 1: bfloat16 [4096, 32768], P(None, 'ga')
- output 2: float32 [4096], replicated
All inputs are finite; a program needn't handle non-finite values.
Results may differ from a plain program's by a relative error of at most 0.001.
Values are sent between devices in bfloat16 or wider.
A program may use at most 1 GiB of HBM per device.

v0:
```python
import jax
import jax.numpy as jnp
from jax import lax
from jax.sharding import PartitionSpec as P, NamedSharding


def solution(mesh):
    num_dev = mesh.shape["ga"]

    def per_device(text_states, text_proj, gallery, logit_scale):
        proj_out = jnp.dot(text_states, text_proj, preferred_element_type=jnp.float32)
        unit_q = proj_out / jnp.sqrt(jnp.sum(proj_out * proj_out, axis=1, keepdims=True))
        query_emb = unit_q.astype(jnp.bfloat16)
        all_queries = lax.all_gather(query_emb, "ga", axis=0, tiled=True)
        logit_mult = jnp.exp(logit_scale[0])
        scores = logit_mult * lax.dot_general(all_queries, gallery, (((1,), (1,)), ((), ())),
                                              preferred_element_type=jnp.float32)
        glob_max = lax.pmax(jnp.max(scores, axis=1), "ga")
        exp_vals = jnp.exp(scores - glob_max[:, None])
        glob_sum = lax.psum(jnp.sum(exp_vals, axis=1), "ga")
        prob_vals = exp_vals / glob_sum[:, None]
        local_rows = gallery.shape[0]
        total_rows = local_rows * num_dev
        row_ids = lax.axis_index("ga") * local_rows + jnp.arange(local_rows, dtype=jnp.int32)
        positions = row_ids.astype(jnp.float32) / total_rows
        exp_rank = lax.psum(jnp.sum(prob_vals * positions, axis=1), "ga")
        return prob_vals.astype(jnp.bfloat16), exp_rank

    return jax.shard_map(per_device, mesh=mesh,
                         in_specs=(P("ga", None), P(None, None), P("ga", None), P(None)),
                         out_specs=(P(None, "ga"), P(None)), check_vma=False)
```

profile of v0, /device:TPU:0, one launch (start us, length us, event | category | flops | bytes accessed | tf_op | source)
XLA Modules:
  0.0 235.8 jit_solution(9535852909100743798)
XLA Ops:
  7.2 0.0 copy-start
  7.2 0.0 all-gather.2.cloned.1.call-start
  7.2 2.1 multiply_reduce_fusion.2
  9.3 0.9 divide_convert_fusion
  10.2 0.0 all-gather.2.cloned.1.call-update
  10.9 44.5 %all-gather.2.cloned.1.call-done = bf16[4096,768]{1,0:T(8,128)(2,1)} async-done(((bf16[256,768]{1,0:T(8,128)(2,1)}), bf16[4096,768]{1,0:T(8,128)(2,1)}) %all-gather.2.cloned.1.call-update) | async-done | bytes 6291472 | tf_op jit(solution)/shard_map/all_gather | solution.py:14
  55.4 0.0 copy-done
  55.4 19.9 %multiply_reduce_fusion.1 = (f32[4096]{0:T(1024)S(1)}, f32[4096,2048]{0,1:T(8,128)}) fusion(f32[]{:T(128)} %bitcast, bf16[4096,768]{1,0:T(8,128)(2,1)} %all-gather.2.cloned.1.call-done, bf16[2048,768]{1,0:T(8,128)(2,1)S(1)} %copy-done), kind=kOutput, calls=%fused_computation.2 | convolution fusion | flops 12901675008 | bytes 43008004 | tf_op jit(solution)/shard_map/dot_general | solution.py:16
  75.3 31.9 %pmax.7 = f32[4096]{0:T(1024)S(1)} all-reduce(f32[4096]{0:T(1024)S(1)} %get-tuple-element.8), channel_id=1, replica_groups=mesh['ga'=16] {'ga'}, use_global_device_ids=true, to_apply=%region_2.0 | all-reduce | flops 4096 | bytes 32768 | tf_op jit(solution)/shard_map/pmax | solution.py:18
  107.2 13.7 %fusion.1 = f32[4096]{0:T(1024)S(1)} fusion(f32[4096,2048]{0,1:T(8,128)} %get-tuple-element.9, f32[4096]{0:T(1024)S(1)} %pmax.7, f32[]{:T(128)} %bitcast), kind=kLoop, calls=%fused_computation.4 | loop fusion | flops 25161728 | bytes 33587204 | tf_op jit(solution)/shard_map/reduce_sum | solution.py:20
  120.9 0.0 copy-start.1
  120.9 32.8 %psum.14 = f32[4096]{0:T(1024)S(1)} all-reduce(f32[4096]{0:T(1024)S(1)} %fusion.1), channel_id=1, replica_groups=mesh['ga'=16] {'ga'}, use_global_device_ids=true, to_apply=%region_4.0 | all-reduce | flops 4096 | bytes 32768 | tf_op jit(solution)/shard_map/psum | solution.py:20
  153.7 20.3 %multiply_reduce_fusion = (f32[4096]{0:T(1024)S(1)}, bf16[4096,2048]{0,1:T(8,128)(2,1)}) fusion(f32[2048]{0:T(1024)S(1)} %convert_multiply_fusion, f32[4096]{0:T(1024)S(1)} %psum.14, f32[4096]{0:T(1024)S(1)} %pmax.7, f32[4096,2048]{0,1:T(8,128)} %get-tuple-element.9, f32[]{:T(128)} %bitcast), kind=kLoop, calls=%fused_computation | loop fusion | flops 50327552 | bytes 50388996 | tf_op jit(solution)/shard_map/reduce_sum | solution.py:26
  173.9 32.6 %psum.15 = f32[4096]{0:T(1024)} all-reduce(f32[4096]{0:T(1024)S(1)} %get-tuple-element.4), channel_id=1, replica_groups=mesh['ga'=16] {'ga'}, use_global_device_ids=true, to_apply=%region_6.0 | all-reduce | flops 4096 | bytes 32768 | tf_op jit(solution)/shard_map/psum | solution.py:26
  206.6 22.4 %copy.6 = bf16[4096,2048]{1,0:T(8,128)(2,1)} copy(bf16[4096,2048]{0,1:T(8,128)(2,1)} %get-tuple-element.5) | data formatting | bytes 33554432
  229.0 0.0 copy-done.1
  (2 shorter events, 0.0 us)
Async XLA Ops:
  7.2 48.3 %copy-start = (bf16[2048,768]{1,0:T(8,128)(2,1)S(1)}, bf16[2048,768]{1,0:T(8,128)(2,1)}, u32[]{:S(2)}) copy-start(bf16[2048,768]{1,0:T(8,128)(2,1)} %param.6) | copy-start | bytes 9437188
  7.2 48.2 %all-gather.2.cloned.1.call-start = ((), (), s32[]{:S(2)}) async-start(), calls=%async_computation | async-start | bytes 6684672 | tf_op jit(solution)/shard_map/all_gather | solution.py:14
  120.9 108.1 %copy-start.1 = (bf16[2048,768]{1,0:T(8,128)(2,1)S(1)}, bf16[2048,768]{1,0:T(8,128)(2,1)}, u32[]{:S(2)}) copy-start(bf16[2048,768]{1,0:T(8,128)(2,1)} %param.6) | copy-start | bytes 9437188
Sparse Core Ops, SparseCore 0:
  10.8 44.5 all-gather.1
where the time goes:
time: 237 us; the launch traced here: 236 us
  blocking collectives  97.2 us (41%)
  waiting for transfers between devices  44.5 us (19%)
  other arithmetic  34.9 us (15%)
  local copies, waits for them, and re-layouts  22.5 us (9%)
  matrix products  22 us (9%)
  between operations  14.7 us (6%)
    all_gather x1, waiting for transfers between devices, per_device(): all_queries = lax.all_gather(query_emb, 'ga', axis=0, tiled=True)  44.5 us
    psum x1, blocking collectives, per_device(): glob_sum = lax.psum(jnp.sum(exp_vals, axis=1), 'ga')  32.8 us
    psum x1, blocking collectives, per_device(): exp_rank = lax.psum(jnp.sum(prob_vals * positions, axis=1), 'ga')  32.6 us
    pmax x1, blocking collectives, per_device(): glob_max = lax.pmax(jnp.max(scores, axis=1), 'ga')  31.9 us
    unnamed x5, local copies, waits for them, and re-layouts  22.4 us
    reduce_sum x1, other arithmetic, per_device(): exp_rank = lax.psum(jnp.sum(prob_vals * positions, axis=1), 'ga')  20.3 us
    dot_general x1, matrix products, per_device(): lax.dot_general(all_queries, gallery, (((1,), (1,)), ((), ())), preferred...  19.9 us
    reduce_sum x1, other arithmetic, per_device(): glob_sum = lax.psum(jnp.sum(exp_vals, axis=1), 'ga')  13.7 us
  transfers between devices with their start and end apart: 1, of which 1 were waited for; matrix products, arithmetic and copies ran while one was open for 0% of the time, Pallas kernels for 0%

commit v1 on v0

v1 whole, which is shorter than its diff:
```python
import functools

import jax
import jax.numpy as jnp
from jax import lax
from jax.experimental import pallas as pl
from jax.experimental.pallas import tpu as pltpu
from jax.sharding import PartitionSpec as P

MESH = pl.DeviceIdType.MESH
LOG2E = 1.4426950408889634
F32_MAX = 3.4028234663852886e38

LEN = (96, 80, 80)
OFF = (0, 96, 176)
ROWS = 256
COLS = 2048
EMB = 768
LANES = 128
TILES = COLS // LANES


def source_mask(slot, k):
    a, b, c = 1 << k, 1 << ((k + 1) % 3), 1 << ((k + 2) % 3)
    return (0, a, b, c, a | b, a | c, b | c, 7)[slot]


def slot_of(mask, k):
    return next(s for s in range(8) if source_mask(s, k) == mask)


def relative(dev, v, h):
    out = dev
    for bit, weight in ((h, 1), (v & 1, 2), (v >> 1 & 1, 4), (v >> 2 & 1, 8)):
        if bit:
            out = out + weight * (1 - 2 * ((dev // weight) % 2))
    return out


def scale_row(t_ref):
    mult = jnp.exp(jnp.full((8, LANES), t_ref[0], jnp.float32))
    return jnp.minimum(mult * LOG2E, F32_MAX)[0:1, :]


def score_kernel(t_ref, x_hbm, w_hbm, g_hbm, e0, e1, ml0, ml1, fin_out, rank_out,
                 xv, wv, gv, q0, q1, s_acc, r_acc, cst, snd, rst, mine, fin,
                 ld_sem, pair_s, pair_r, link_s, link_r, st_s, st_r, fb_s, fb_r):
    dev = lax.axis_index("ga")
    e, ml, q = (e0, e1), (ml0, ml1), (q0, q1)

    loads = [pltpu.make_async_copy(src, dst, ld_sem.at[i])
             for i, (src, dst) in enumerate(((x_hbm, xv), (w_hbm, wv), (g_hbm, gv)))]
    for load in loads:
        load.start()
    barrier = pltpu.get_barrier_semaphore()
    for other in range(1, 16):
        pl.semaphore_signal(barrier, inc=1, device_id=(relative(dev, other >> 1, other & 1),), device_id_type=MESH)

    cc = scale_row(t_ref)
    lane = lax.broadcasted_iota(jnp.int32, (8, LANES), 1)
    pos = ((dev * COLS + lane).astype(jnp.float32) * (1.0 / (16 * COLS)))[0:1, :]

    loads[0].wait()
    loads[1].wait()
    u = jnp.dot(xv[...], wv[...], preferred_element_type=jnp.float32)
    inv = 1.0 / jnp.sqrt(jnp.sum(u * u, axis=1, keepdims=True))
    q0[0] = (u * inv).astype(jnp.bfloat16)
    pl.semaphore_wait(barrier, 15)

    def pair_copy(slot):
        return pltpu.make_async_remote_copy(
            src_ref=q0.at[slot], dst_ref=q1.at[slot], send_sem=pair_s.at[slot], recv_sem=pair_r.at[slot],
            device_id=(relative(dev, 0, 1),), device_id_type=MESH)

    def link_copy(slot, src_slot, k):
        d = {1: k, 2: k + 1, 3: k + 2, 4: k + 1, 5: k + 2, 6: k + 2, 7: k + 2}[slot] % 3
        rows = pl.ds(OFF[k], LEN[k])
        return pltpu.make_async_remote_copy(
            src_ref=q0.at[src_slot, rows], dst_ref=q0.at[slot, rows],
            send_sem=link_s.at[slot * 3 + k], recv_sem=link_r.at[slot * 3 + k],
            device_id=(relative(dev, 1 << d, 0),), device_id_type=MESH)

    def wait_link(slot):
        for k in range(3):
            rows = pl.ds(OFF[k], LEN[k])
            pltpu.make_async_remote_copy(
                src_ref=q0.at[slot, rows], dst_ref=q0.at[slot, rows],
                send_sem=link_s.at[slot * 3 + k], recv_sem=link_r.at[slot * 3 + k],
                device_id=(relative(dev, 0, 1),), device_id_type=MESH).wait_recv()

    for slot in (1, 2, 3):
        for k in range(3):
            link_copy(slot, 0, k).start()
    pair_copy(0).start()
    loads[2].wait()

    def body(mm, ex, st):
        for i in range(4):
            if mm is not None:
                slot, h = mm
                s = lax.dot_general(q[h][slot], gv[512 * i:512 * (i + 1), :], (((1,), (1,)), ((), ())),
                                    preferred_element_type=jnp.float32)
                e[h][slot, :, 512 * i:512 * (i + 1)] = s
                m = jnp.maximum(jnp.maximum(s[:, 0:128], s[:, 128:256]), jnp.maximum(s[:, 256:384], s[:, 384:512]))
                ml[h][slot] = m if i == 0 else jnp.maximum(ml[h][slot], m)
            if ex is not None:
                slot, h = ex
                rows = slice(64 * i, 64 * (i + 1))
                m = ml[h][slot, rows, :]
                total = jnp.zeros((64, LANES), jnp.float32)
                ranked = jnp.zeros((64, LANES), jnp.float32)
                for j in reversed(range(TILES)):
                    cols = slice(LANES * j, LANES * (j + 1))
                    v = jnp.exp2((e[h][slot, rows, cols] - m) * cc)
                    e[h][slot, rows, cols] = v
                    ranked = ranked + total
                    total = total + v
                s_acc[h, rows, :] = total
                r_acc[h, rows, :] = ranked * (1.0 / (16 * TILES)) + total * pos
        if st is not None:
            slot, h = st
            for half in range(2):
                rows = slice(128 * half, 128 * (half + 1))
                mt = ml[h][slot, rows, :].T
                top = jnp.max(mt, axis=0, keepdims=True)
                w = jnp.exp2((mt - top) * cc)
                cst[slot, h, half:half + 1, :] = top
                cst[slot, h, 2 + half:3 + half, :] = jnp.sum(s_acc[h, rows, :].T * w, axis=0, keepdims=True)
                cst[slot, h, 4 + half:5 + half, :] = jnp.sum(r_acc[h, rows, :].T * w, axis=0, keepdims=True)

    body((0, 0), None, None)
    pair_copy(0).wait_recv()
    body((0, 1), (0, 0), None)

    def step(t, carry):
        wait_link_dyn(t)
        pair_dyn(t).start()

        @pl.when(t == 1)
        def _():
            for slot in (4, 5):
                for k in range(3):
                    link_copy(slot, 1, k).start()

        @pl.when(t == 2)
        def _():
            for k in range(3):
                link_copy(6, 2, k).start()

        @pl.when(t == 4)
        def _():
            for k in range(3):
                link_copy(7, 4, k).start()

        body((t, 0), (t - 1, 1), (t - 1, 0))
        pair_dyn(t).wait_recv()
        body((t, 1), (t, 0), (t - 1, 1))
        return carry

    wait_link_dyn, pair_dyn = wait_link, pair_copy
    lax.fori_loop(1, 8, step, 0)

    row = lax.broadcasted_iota(jnp.int32, (8, LANES), 0)
    lane8 = lax.broadcasted_iota(jnp.int32, (8, LANES), 1)
    query = (row % 2) * LANES + lane8
    first, second = query < OFF[1], query < OFF[2]

    def st_copy(v, h):
        i = 2 * (v ^ 7) + h
        return pltpu.make_async_remote_copy(
            src_ref=snd.at[i], dst_ref=rst.at[i], send_sem=st_s.at[i], recv_sem=st_r.at[i],
            device_id=(relative(dev, v ^ 7, h),), device_id_type=MESH)

    for v in range(7):
        for h in range(2):
            tiles = [cst[slot_of(v, k), h] for k in range(3)]
            snd[2 * (v ^ 7) + h] = jnp.where(first, tiles[0], jnp.where(second, tiles[1], tiles[2]))
    for v in range(7):
        for h in range(2):
            st_copy(v, h).start()

    body(None, (7, 1), (7, 0))
    body(None, None, (7, 1))
    snd[1] = cst[7, 1]
    st_copy(7, 1).start()

    def fb_copy(v, h):
        i = 2 * (v ^ 7) + h
        return pltpu.make_async_remote_copy(
            src_ref=mine, dst_ref=fin.at[i], send_sem=fb_s.at[i], recv_sem=fb_r.at[i],
            device_id=(relative(dev, v, h),), device_id_type=MESH)

    for v in range(8):
        for h in range(2):
            if v ^ 7 or h:
                st_copy(v, h).wait_recv()
    parts = [cst[7, 0]] + [rst[i] for i in range(1, 16)]
    top = functools.reduce(jnp.maximum, [part[0:2] for part in parts])
    total = jnp.zeros((2, LANES), jnp.float32)
    ranked = jnp.zeros((2, LANES), jnp.float32)
    for part in parts:
        w = jnp.exp2((part[0:2] - top) * cc)
        total = total + part[2:4] * w
        ranked = ranked + part[4:6] * w
    scale = 1.0 / total
    mine[0:2, :] = top
    mine[2:4, :] = scale
    mine[4:6, :] = ranked * scale
    mine[6:8, :] = jnp.zeros((2, LANES), jnp.float32)
    for v in range(8):
        for h in range(2):
            if v or h:
                fb_copy(v, h).start()
    fin[14] = mine[...]
    for v in range(8):
        for h in range(2):
            if v or h:
                fb_copy(v, h).wait_recv()
    for slot in range(8):
        for h in range(2):
            tiles = [fin[2 * source_mask(slot, k) + h] for k in range(3)]
            fin_out[slot, h] = jnp.where(first, tiles[0], jnp.where(second, tiles[1], tiles[2]))
    rank_out[...] = fin[...]

    for slot in range(8):
        pair_copy(slot).wait_send()
    for slot, src in ((1, 0), (2, 0), (3, 0), (4, 1), (5, 1), (6, 2), (7, 4)):
        for k in range(3):
            link_copy(slot, src, k).wait_send()
    for v in range(8):
        for h in range(2):
            if v ^ 7 or h:
                st_copy(v, h).wait_send()
            if v or h:
                fb_copy(v, h).wait_send()


NBUF = 3


def write_kernel(t_ref, e0, e1, ml0, ml1, fin, rank, p_hbm, r_out, stage, fac, sems):
    dev = lax.axis_index("ga")
    cc = scale_row(t_ref)
    for v in range(8):
        for h in range(2):
            r_out[pl.ds(2 * relative(dev, v, h), 2), :] = rank[2 * v + h, 4:6, :]

    def out_copy(slot, h, k, buf):
        v = jnp.int32(source_mask(0, k))
        for s in range(1, 8):
            v = jnp.where(slot == s, source_mask(s, k), v)
        src = dev
        for i, weight in ((0, 2), (1, 4), (2, 8)):
            src = src + (v // (1 << i)) % 2 * weight * (1 - 2 * ((dev // weight) % 2))
        if h:
            src = src + (1 - 2 * (dev % 2))
        row = pl.multiple_of(src * ROWS + OFF[k], 16)
        return pltpu.make_async_copy(stage.at[buf, pl.ds(OFF[k], LEN[k])], p_hbm.at[pl.ds(row, LEN[k])], sems.at[buf, k])

    def do_block(slot, h, n):
        buf = lax.rem(n, NBUF)

        @pl.when(n >= NBUF)
        def _():
            for k in range(3):
                out_copy(0, 0, k, buf).wait()

        eb, mb = (e0, e1)[h], (ml0, ml1)[h]
        for half in range(2):
            rows = slice(128 * half, 128 * (half + 1))
            top = jnp.broadcast_to(fin[slot, h, half:half + 1, :], (LANES, LANES)).T
            inv = jnp.broadcast_to(fin[slot, h, 2 + half:3 + half, :], (LANES, LANES)).T
            fac[rows, :] = jnp.exp2((mb[slot, rows, :] - top) * cc) * inv

        for k in range(3):
            for r in range(OFF[k], OFF[k] + LEN[k], 16):
                f = fac[r:r + 16, :]
                for j in range(TILES):
                    cols = slice(LANES * j, LANES * (j + 1))
                    stage[buf, r:r + 16, cols] = (eb[slot, r:r + 16, cols] * f).astype(jnp.bfloat16)
            out_copy(slot, h, k, buf).start()

    def step(t, carry):
        do_block(t, 0, 2 * t)
        do_block(t, 1, 2 * t + 1)
        return carry

    lax.fori_loop(0, 8, step, 0)
    for n in range(16 - NBUF, 16):
        for k in range(3):
            out_copy(0, 0, k, n % NBUF).wait()


def solution(mesh):
    vmem = pl.BlockSpec(memory_space=pltpu.VMEM)
    hbm = pl.BlockSpec(memory_space=pl.ANY)
    smem = pl.BlockSpec(memory_space=pltpu.SMEM)
    f32, bf16 = jnp.float32, jnp.bfloat16

    def per_device(text_states, text_proj, gallery, logit_scale):
        e0, e1, ml0, ml1, fin, rank = pl.pallas_call(
            score_kernel,
            out_shape=(
                pltpu.VMEM((8, ROWS, COLS), f32), pltpu.VMEM((8, ROWS, COLS), f32),
                pltpu.VMEM((8, ROWS, LANES), f32), pltpu.VMEM((8, ROWS, LANES), f32),
                pltpu.VMEM((8, 2, 8, LANES), f32), pltpu.VMEM((16, 8, LANES), f32),
            ),
            in_specs=[smem, hbm, hbm, hbm],
            out_specs=(vmem,) * 6,
            scratch_shapes=[
                pltpu.VMEM((ROWS, EMB), bf16), pltpu.VMEM((EMB, EMB), bf16), pltpu.VMEM((COLS, EMB), bf16),
                pltpu.VMEM((8, ROWS, EMB), bf16), pltpu.VMEM((8, ROWS, EMB), bf16),
                pltpu.VMEM((2, ROWS, LANES), f32), pltpu.VMEM((2, ROWS, LANES), f32),
                pltpu.VMEM((8, 2, 8, LANES), f32), pltpu.VMEM((16, 8, LANES), f32), pltpu.VMEM((16, 8, LANES), f32),
                pltpu.VMEM((8, LANES), f32), pltpu.VMEM((16, 8, LANES), f32),
                pltpu.SemaphoreType.DMA((3,)), pltpu.SemaphoreType.DMA((8,)), pltpu.SemaphoreType.DMA((8,)),
                pltpu.SemaphoreType.DMA((24,)), pltpu.SemaphoreType.DMA((24,)),
                pltpu.SemaphoreType.DMA((16,)), pltpu.SemaphoreType.DMA((16,)),
                pltpu.SemaphoreType.DMA((16,)), pltpu.SemaphoreType.DMA((16,)),
            ],
            compiler_params=pltpu.CompilerParams(collective_id=0, has_side_effects=True,
                                                 vmem_limit_bytes=26 * 1024 * 1024),
            name="score",
        )(logit_scale, text_states, text_proj, gallery)
        e0, e1, ml0, ml1, fin, rank = (pltpu.with_memory_space_constraint(a, pltpu.VMEM)
                                       for a in (e0, e1, ml0, ml1, fin, rank))
        prob, ranks = pl.pallas_call(
            write_kernel,
            out_shape=(jax.ShapeDtypeStruct((16 * ROWS, COLS), bf16), jax.ShapeDtypeStruct((32, LANES), f32)),
            in_specs=[smem] + [vmem] * 6,
            out_specs=(hbm, vmem),
            scratch_shapes=[pltpu.VMEM((NBUF, ROWS, COLS), bf16), pltpu.VMEM((ROWS, LANES), f32),
                            pltpu.SemaphoreType.DMA((NBUF, 3))],
            compiler_params=pltpu.CompilerParams(vmem_limit_bytes=26 * 1024 * 1024),
            name="write",
        )(logit_scale, e0, e1, ml0, ml1, fin, rank)
        return prob, ranks.reshape(32 * LANES)

    return jax.shard_map(per_device, mesh=mesh,
                         in_specs=(P("ga", None), P(None, None), P("ga", None), P(None)),
                         out_specs=(P(None, "ga"), P(None)), check_vma=False)
```

time: 237 us -> 47.7 us (0.20)
  blocking collectives: 97.2 us -> 0 us
  Pallas kernels: 0 us -> 46.3 us
  waiting for transfers between devices: 44.5 us -> 0 us
  other arithmetic: 34.9 us -> 0 us
  local copies, waits for them, and re-layouts: 22.5 us -> 0 us
  matrix products: 22 us -> 0 us
  between operations: 14.7 us -> 1.29 us
    psum x2 -> x0, blocking collectives: 65.4 us -> none  [the longest x1 32.8 us: per_device(): glob_sum = lax.psum(jnp.sum(exp_vals, axis=1), 'ga')]
    pallas_call x0 -> x2, Pallas kernels: none -> 46.3 us  [the longest x1 39 us: per_device(): pl.pallas_call(score_kernel, out_shape=(pltpu.VMEM((8, ROWS, COLS), f32),...]
    all_gather x1 -> x0, waiting for transfers between devices: 44.5 us -> none  [per_device(): all_queries = lax.all_gather(query_emb, 'ga', axis=0, tiled=True)]
    reduce_sum x2 -> x0, other arithmetic: 34 us -> none  [the longest x1 20.3 us: per_device(): exp_rank = lax.psum(jnp.sum(prob_vals * positions, axis=1), 'ga')]
    pmax x1 -> x0, blocking collectives: 31.9 us -> none  [per_device(): glob_max = lax.pmax(jnp.max(scores, axis=1), 'ga')]
    unnamed x5 -> x0, local copies, waits for them, and re-layouts: 22.4 us -> none
    dot_general x2 -> x0, matrix products: 22 us -> none  [the longest x1 19.9 us: per_device(): lax.dot_general(all_queries, gallery, (((1,), (1,)), ((), ())), preferred...]
  transfers between devices with their start and end apart: 1 -> 0, of which waited for: 1 -> 0; matrix products, arithmetic and copies ran while one was open for 0% -> 0% of each run, Pallas kernels for 0% -> 0%
where the time goes in v1:
time: 47.7 us; the launch traced here: 47.6 us
  Pallas kernels  46.3 us (97%)
  between operations  1.29 us (3%)
    pallas_call x1, Pallas kernels, per_device(): pl.pallas_call(score_kernel, out_shape=(pltpu.VMEM((8, ROWS, COLS), f32),...  39 us
    pallas_call x1, Pallas kernels, per_device(): pl.pallas_call(write_kernel, out_shape=(jax.ShapeDtypeStruct((16 * ROWS,...  7.29 us

profile of v1, /device:TPU:0, one launch (start us, length us, event | category | flops | bytes accessed | tf_op | source)
XLA Modules:
  0.0 47.6 jit_solution(10454507509410042295)
XLA Ops:
  1.3 39.0 %score.1 = (f32[8,256,2048]{2,1,0:T(8,128)S(1)}, f32[8,256,2048]{2,1,0:T(8,128)S(1)}, f32[8,256,128]{2,1,0:T(8,128)S(1)}, f32[8,256,128]{2,1,0:T(8,128)S(1)}, f3...) custom-call(f32[1]{0:T(128)S(6)} %copy.6.t_ref, bf16[256,768]{1,0:T(8,128)(2,1)} %x_hbm.1, bf16[768,768]{1,0:T(8,128)(2,1)} %w_hbm.1, ...), custom_call_target="tpu_custom_call" | custom-call | tf_op jit(solution)/shard_map/score/pallas_call | solution.py:301
  40.3 7.3 %write.1 = (bf16[4096,2048]{1,0:T(8,128)(2,1)}, f32[32,128]{1,0:T(8,128)}) custom-call(f32[1]{0:T(128)S(6)} %copy.6.t_ref, f32[8,256,2048]{2,1,0:T(8,128)S(1)} %get-tuple-element.10.e0, f32[8,256,2048]{2,1,0:T(8,128)S(1)} %get-tuple-element.11.e1, f32[8,256,128]{2,1,0:T(8,128)S(1)} %get-tuple-element.12.ml0, f32[8,256,128]{2,1,0:T(8,128)S(1)} %get-tuple-element.13.ml1, ...), custom_call_target="tpu_custom_call" | custom-call | tf_op jit(solution)/shard_map/write/pallas_call | solution.py:327
